TPU v7x, 256 devices: a whole 4x4x8 slice. The times are simulated.
256 devices in a mesh: row: 16 (over z, x_lo), col: 16 (over y, x_hi, core).
Axes of the slice: x: 4 (x_hi: 2, x_lo: 2; x = x_hi * 2 + x_lo), y: 4, z: 8, core: 2. Of those that a mesh axis runs over, the one named last changes fastest.
Arguments:
- matrix: float32 [512, 32, 128, 128], P('row', 'col'), may hold values from -0.09375 to 0.09375
- columns: int32 [512, 32], P('row', 'col'), may hold values from 0 to 31
- counts: int32 [512, 16], P('row', 'col'), may hold values from 1 to 2
- fine_guess: float32 [512, 32, 128], P(('col', 'row')), may hold values from -6 to 6
- right_side: float32 [512, 32, 128], P(('row', 'col')), may hold values from -6 to 6
- aggregate: int32 [512], P(('row', 'col')), may hold values from 0 to 7
- restrict: float32 [512, 128, 128], P(('row', 'col')), may hold values from -0.5 to 0.5
Outputs:
- coarse_scaled: float32 [128, 32, 128], P('row')
- residual: float32 [512, 32, 128], P(('row', 'col'))
Inputs may be any that keep to these rules, and one draw needn't show every extreme that they name: `counts`: slots at or past the count hold no part of the operator.
All inputs are finite; a program needn't handle non-finite values.
Results may differ from a plain program's by a relative error of at most 0.000071.
Values sent between devices are 32-bit elements; how exact they have to be, the bound alone decides.
A program may use at most 64 MiB of HBM per device.

v0:
```python
import jax
import jax.numpy as jnp
from jax import lax
from jax.sharding import PartitionSpec as P

NC_GRP = 8


def sent_to_all(x, axis):
    length = lax.axis_size(axis)
    return lax.all_to_all(jnp.broadcast_to(x[None], (length, *x.shape)), axis, 0, 0, tiled=True)


def laid_out(blocks, dim):
    shape = list(blocks.shape[1:])
    shape[dim] *= blocks.shape[0]
    return jnp.moveaxis(blocks, 0, dim).reshape(shape)


def gathered_copies(x, axis, dim):
    blocks = sent_to_all(x, axis)
    return laid_out(blocks, dim)


def cut_along(x, dim, length):
    shape = x.shape
    blocks = x.reshape(*shape[:dim], length, shape[dim] // length, *shape[dim + 1 :])
    return jnp.moveaxis(blocks, dim, 0)


def summed_on_arrival(x, axis, dim):
    length = lax.axis_size(axis)
    blocks = lax.all_to_all(cut_along(x, dim, length), axis, 0, 0, tiled=True)
    return jnp.sum(blocks, axis=0)


def over_copies(x, axis):
    everything = sent_to_all(x, axis)
    return jnp.sum(everything, axis=0)


def packed_total(arrays, axis):
    ends = [0]
    for a in arrays:
        ends.append(ends[-1] + a.size)
    total = over_copies(jnp.concatenate([a.ravel() for a in arrays]), axis)
    return tuple((total[b:e].reshape(a.shape) for a, b, e in zip(arrays, ends, ends[1:])))


def local(matrix, columns, counts, fine_guess, right_side, aggregate, restrict):
    column_vector = gathered_copies(fine_guess, "row", 0)
    slot_count = matrix.shape[1]
    usable = jnp.arange(slot_count, dtype=jnp.int32)[None, :] < counts
    picked = jnp.take(column_vector, columns, axis=0) * usable[:, :, None, None].astype(jnp.float32)
    partial_value = jnp.einsum("gsab,gsvb->gva", matrix, picked, precision=lax.Precision.HIGHEST)
    product = summed_on_arrival(partial_value, "col", 0)
    residual = right_side - product
    contrib = jnp.einsum("gva,gak->gvk", residual, restrict, precision=lax.Precision.HIGHEST)
    onehot = (aggregate[:, None] == jnp.arange(NC_GRP, dtype=jnp.int32)[None, :]).astype(
        jnp.float32
    )
    coarse_part = jnp.einsum("gc,gvk->cvk", onehot, contrib, precision=lax.Precision.HIGHEST)
    squares = jnp.sum(residual * residual, axis=(0, 2))
    coarse, group_sq = packed_total((coarse_part, squares), "col")
    total_sq = over_copies(group_sq, "row")
    entries = residual.shape[0] * residual.shape[2] * lax.axis_size("row") * lax.axis_size("col")
    scale_rms = jnp.sqrt(total_sq / entries + 1e-06)
    return (coarse / scale_rms[None, :, None], residual)


def solution(mesh):
    in_specs = (
        P("row", "col", None, None),
        P("row", "col"),
        P("row", "col"),
        P(("col", "row"), None, None),
        P(("row", "col"), None, None),
        P(("row", "col")),
        P(("row", "col"), None, None),
    )
    out_specs = (P("row", None, None), P(("row", "col"), None, None))
    return jax.shard_map(local, mesh=mesh, in_specs=in_specs, out_specs=out_specs, check_vma=False)
```

profile of v0, /device:TPU:1, one launch (start us, length us, event | category | flops | bytes accessed | tf_op | source)
XLA Modules:
  0.0 103.1 jit_solution(11516528413000711896)
XLA Ops:
  0.6 0.0 copy-start
  0.6 1.6 %broadcast_in_dim.19 = f32[16,2,32,128]{3,2,1,0:T(8,128)} broadcast(f32[2,32,128]{2,1,0:T(8,128)} %param.10), dimensions={1,2,3} | broadcast | bytes 557056 | tf_op jit(solution)/shard_map/broadcast_in_dim | solution.py:11
  2.3 10.0 %all-to-all-start = ((f32[16,2,32,128]{3,2,1,0:T(8,128)}), f32[16,2,32,128]{3,2,1,0:T(8,128)S(1)}, u32[]{:S(2)}, u32[]{:S(2)}) async-start(f32[16,2,32,128]{3,2,1,0:T(8,128)} %broadcast_in_dim.19), calls=%async_computation | async-start | bytes 1048576 | tf_op jit(solution)/shard_map/all_to_all | solution.py:11
  12.3 0.7 compare_and_fusion
  13.0 0.1 copy.18
  13.1 0.7 compare_select_fusion
  13.8 0.1 copy.19
  13.9 0.1 reshape.70
  14.0 0.7 fusion.8
  14.7 13.3 %all-to-all-done = f32[16,2,32,128]{3,2,1,0:T(8,128)S(1)} async-done(((f32[16,2,32,128]{3,2,1,0:T(8,128)}), f32[16,2,32,128]{3,2,1,0:T(8,128)S(1)}, u32[]{:S(2)}, u32[]{:S(2)}) %all-to-all-start) | async-done | bytes 524320 | tf_op jit(solution)/shard_map/all_to_all | solution.py:11
  28.0 0.6 gather_fusion
  28.7 0.0 copy-start.2
  28.7 0.0 copy-start.3
  28.7 6.2 %fusion = f32[32,32,128,1]{2,1,3,0:T(8,128)S(1)} fusion(f32[32,2,128,128]{3,2,1,0:T(8,128)} %param.7, f32[32,2,32,128]{3,2,1,0:T(8,128)S(1)} %bitcast.17, f32[32,2]{1,0:T(8,128)S(1)} %fusion.8, pred[32,2]{1,0:T(8,128)(4,1)S(1)} %copy.18), kind=kOutput, calls=%fused_computation.1 | convolution fusion | flops 403177472 | bytes 5767488 | tf_op jit(solution)/shard_map/gsab,gsvb->gva/dot_general | solution.py:55
  34.9 20.2 %all_to_all.22 = f32[16,2,32,128]{3,2,1,0:T(8,128)S(1)} all-to-all(f32[16,2,32,128]{3,2,1,0:T(8,128)S(1)} %bitcast.18), channel_id=1, replica_groups=mesh['row'=16,'col'=16] {'col'}, dimensions={0} | all-to-all | bytes 1048576 | tf_op jit(solution)/shard_map/all_to_all | solution.py:33
  55.1 0.0 copy-done.2
  55.1 0.1 multiply_reduce_fusion
  55.2 0.0 copy-start.1
  55.2 0.0 copy-done
  55.2 0.2 fusion.14
  55.5 0.0 copy-done.3
  55.5 0.3 fusion.6
  55.9 1.1 %broadcast_in_dim.22 = f32[16,1,32800]{2,1,0:T(1,128)S(1)} broadcast(f32[32800]{0:T(1024)S(1)} %pad_maximum_fusion), dimensions={2} | broadcast | bytes 2230400 | tf_op jit(solution)/shard_map/broadcast_in_dim | solution.py:11
  56.9 32.7 %all_to_all.23 = f32[16,1,32800]{2,1,0:T(1,128)S(1)} all-to-all(f32[16,1,32800]{2,1,0:T(1,128)S(1)} %broadcast_in_dim.22), channel_id=1, replica_groups=mesh['row'=16,'col'=16] {'col'}, dimensions={0} | all-to-all | bytes 4198400 | tf_op jit(solution)/shard_map/all_to_all | solution.py:11
  89.7 1.3 %reduce_sum.38 = f32[32800]{0:T(1024)S(1)} reduce(f32[16,1,32800]{2,1,0:T(1,128)S(1)} %all_to_all.23, f32[]{:T(128)} %constant.20.clone.1), dimensions={0,1}, to_apply=%region_2.3 | reduce | flops 492000 | bytes 2230404 | tf_op jit(solution)/shard_map/reduce_sum | solution.py:39
  91.0 0.0 copy-done.1
  91.0 0.6 broadcast_in_dim.40
  91.6 3.5 %all-to-all-start.3 = ((f32[16,1,32]{2,1,0:T(1,128)}), f32[16,1,32]{2,1,0:T(1,128)S(1)}, u32[]{:S(2)}, u32[]{:S(2)}) async-start(f32[16,1,32]{2,1,0:T(1,128)} %broadcast_in_dim.40), calls=%async_computation.3 | async-start | bytes 16384 | tf_op jit(solution)/shard_map/all_to_all | solution.py:11
  95.1 7.2 %all-to-all-done.3 = f32[16,1,32]{2,1,0:T(1,128)S(1)} async-done(((f32[16,1,32]{2,1,0:T(1,128)}), f32[16,1,32]{2,1,0:T(1,128)S(1)}, u32[]{:S(2)}, u32[]{:S(2)}) %all-to-all-start.3) | async-done | bytes 2080 | tf_op jit(solution)/shard_map/all_to_all | solution.py:11
  102.4 0.7 broadcast_divide_fusion
  (8 shorter events, 0.1 us)
Async XLA Ops:
  0.6 54.6 %copy-start = (f32[2,128,128]{2,1,0:T(8,128)S(1)}, f32[2,128,128]{2,1,0:T(8,128)}, u32[]{:S(2)}) copy-start(f32[2,128,128]{2,1,0:T(8,128)} %param.13) | copy-start | bytes 393220
  2.3 25.7 %all-to-all-start = ((f32[16,2,32,128]{3,2,1,0:T(8,128)}), f32[16,2,32,128]{3,2,1,0:T(8,128)S(1)}, u32[]{:S(2)}, u32[]{:S(2)}) async-start(f32[16,2,32,128]{3,2,1,0:T(8,128)} %broadcast_in_dim.19), calls=%async_computation | async-start | bytes 1048576 | tf_op jit(solution)/shard_map/all_to_all | solution.py:11
  28.7 26.4 %copy-start.2 = (f32[2,32,128]{2,1,0:T(8,128)S(1)}, f32[2,32,128]{2,1,0:T(8,128)}, u32[]{:S(2)}) copy-start(f32[2,32,128]{2,1,0:T(8,128)} %param.11) | copy-start | bytes 98308
  28.7 26.8 %copy-start.3 = (s32[2]{0:T(128)S(1)}, s32[2]{0:T(128)}, u32[]{:S(2)}) copy-start(s32[2]{0:T(128)} %param.12) | copy-start | bytes 28
  55.2 35.8 %copy-start.1 = (f32[2,32,128]{2,1,0:T(8,128)}, f32[2,32,128]{2,1,0:T(8,128)S(1)}, u32[]{:S(2)}) copy-start(f32[2,32,128]{2,1,0:T(8,128)S(1)} %get-tuple-element.3) | copy-start | bytes 98308
  91.6 10.7 %all-to-all-start.3 = ((f32[16,1,32]{2,1,0:T(1,128)}), f32[16,1,32]{2,1,0:T(1,128)S(1)}, u32[]{:S(2)}, u32[]{:S(2)}) async-start(f32[16,1,32]{2,1,0:T(1,128)} %broadcast_in_dim.40), calls=%async_computation.3 | async-start | bytes 16384 | tf_op jit(solution)/shard_map/all_to_all | solution.py:11
where the time goes:
time: 103 us
  blocking collectives  52.9 us (51%)
  waiting for transfers between devices  20.5 us (20%)
  starting transfers between devices  13.5 us (13%)
  matrix products  6.73 us (7%)
  other arithmetic  4.35 us (4%)
  local copies, waits for them, and re-layouts  4.33 us (4%)
    all_to_all x1, blocking collectives, sent_to_all(): lax.all_to_all(jnp.broadcast_to(x[None], (length, *x.shape)), axis, 0, 0,...  32.7 us
    all_to_all x2, waiting for transfers between devices, sent_to_all(): lax.all_to_all(jnp.broadcast_to(x[None], (length, *x.shape)), axis, 0, 0,...  20.5 us
    all_to_all x1, blocking collectives, summed_on_arrival(): blocks = lax.all_to_all(cut_along(x, dim, length), axis, 0, 0, tiled=True)  20.2 us
    all_to_all x2, starting transfers between devices, sent_to_all(): lax.all_to_all(jnp.broadcast_to(x[None], (length, *x.shape)), axis, 0, 0,...  13.5 us
    dot_general x1, matrix products, local(): jnp.einsum('gsab,gsvb->gva', matrix, picked, precision=lax.Precision.HIGH...  6.2 us
    broadcast_in_dim x3, local copies, waits for them, and re-layouts, sent_to_all(): jnp.broadcast_to(x[None], (length, *x.shape))  3.33 us
  transfers between devices with their start and end apart: 2, of which 2 were waited for; matrix products, arithmetic and copies ran while one was open for 2% of the time, Pallas kernels for 0%

commit v1 on v0

v1 whole, which is shorter than its diff:
```python
import jax
import jax.numpy as jnp
from jax import lax
from jax.experimental import pallas as pl
from jax.experimental.pallas import tpu as pltpu
from jax.sharding import PartitionSpec as P

MESH = pl.DeviceIdType.MESH
F32 = jnp.float32
BF16 = jnp.bfloat16

NR, NC = 16, 16
NZ = NR // 2
NQ = NC // 2
GR, KB, NV, BS = 32, 2, 32, 128
NAGG = 8
CHUNKS = 4
Z_ORDER = (4, 3, 5, 2, 6, 1, 7)
Q_ORDER = ((2, 1), (1, 1), (3, 1), (2, 0), (0, 1), (1, 0), (3, 0), (0, 0))


def split(x):
    hi = x.astype(BF16)
    return hi, (x - hi.astype(F32)).astype(BF16)


def kernel(
    mat, cols, cnts, xin, rhs, agg, rest, coarse_out, resid_out,
    mraw, mw, xg, pout, pin, sb, rb, aout, ain, cbuf, sqb, rhs_v, rest_v, tmp, ov,
    cols_s, cnts_s, agg_s,
    mat_sem, loc_sem, ag_send, ag_recv, p_send, p_recv, s_send, s_recv,
    a_send, a_recv, b_send, b_recv, q_send, q_recv, out_sem,
):
    r = lax.axis_index("row")
    c = lax.axis_index("col")
    z, xl = r // 2, r % 2
    core, chip = c % 2, c // 2
    y, xh = chip // 2, chip % 2

    def remote(src, dst, ss, rs, row, col):
        return pltpu.make_async_remote_copy(
            src_ref=src, dst_ref=dst, send_sem=ss, recv_sem=rs,
            device_id=(row, col), device_id_type=MESH,
        )

    own_x = pltpu.make_async_copy(xin, xg.at[pl.ds(2 * r, 2)], loc_sem.at[0])
    own_x.start()
    per = GR // CHUNKS
    mats = [
        pltpu.make_async_copy(mat.at[pl.ds(k * per, per)], mraw.at[pl.ds(k * per, per)], mat_sem.at[k])
        for k in range(CHUNKS)
    ]
    for m in mats:
        m.start()
    smalls = [
        pltpu.make_async_copy(cols, cols_s, loc_sem.at[1]),
        pltpu.make_async_copy(cnts, cnts_s, loc_sem.at[2]),
        pltpu.make_async_copy(agg, agg_s, loc_sem.at[3]),
        pltpu.make_async_copy(rhs, rhs_v, loc_sem.at[4]),
        pltpu.make_async_copy(rest, rest_v, loc_sem.at[5]),
    ]
    for m in smalls:
        m.start()

    barrier = pltpu.get_barrier_semaphore()

    def greet(d, carry):
        pl.semaphore_signal(barrier, inc=1, device_id=((r + d) % NR, c), device_id_type=MESH)
        pl.semaphore_signal(barrier, inc=1, device_id=(r, (c + d) % NC), device_id_type=MESH)
        return carry

    lax.fori_loop(1, 16, greet, 0)
    own_x.wait()
    pl.semaphore_wait(barrier, NR - 1 + NC - 1)

    other = z * 2 + 1 - xl

    def ag(block_row, to_row, s):
        ref = xg.at[pl.ds(2 * block_row, 2)]
        return remote(ref, ref, ag_send.at[s], ag_recv.at[block_row], to_row, c)

    sends = []
    for i, d in enumerate(Z_ORDER):
        cp = ag(r, ((z + d) % NZ) * 2 + xl, i)
        cp.start()
        sends.append(cp)
    cp = ag(r, other, 7)
    cp.start()
    sends.append(cp)

    for k in range(CHUNKS):
        mats[k].wait()

        def parts(g, carry):
            for s in range(KB):
                hi, lo = split(mraw[g, s])
                mw[g, 0:BS, s * BS:(s + 1) * BS] = hi
                mw[g, BS:2 * BS, s * BS:(s + 1) * BS] = lo
            return carry

        lax.fori_loop(k * per, (k + 1) * per, parts, 0)

    for i, d in enumerate(Z_ORDER):
        zr = ((z + NZ - d) % NZ) * 2 + xl
        ag(zr, r, 0).wait_recv()
        cp = ag(zr, other, 8 + i)
        cp.start()
        sends.append(cp)
    for m in smalls:
        m.wait()
    for d in (0,) + Z_ORDER:
        ag(((z + NZ - d) % NZ) * 2 + 1 - xl, r, 0).wait_recv()

    def product(g):
        used = jnp.where(cnts_s[g, 0] > 1, 1.0, 0.0).astype(F32)
        x = jnp.concatenate([xg[cols_s[g, 0]], xg[cols_s[g, 1]] * used], axis=1)
        hi, lo = split(x)
        o = lax.dot_general(
            jnp.concatenate([hi, lo], axis=0), mw[g], (((1,), (1,)), ((), ())),
            preferred_element_type=F32,
        )
        return o[:NV, :BS] + (o[:NV, BS:] + o[NV:, :BS])

    def chip_of(d):
        return ((y + d[0]) % 4) * 2 + (xh + d[1]) % 2

    pair = chip * 2 + 1 - core
    for i, d in enumerate(Q_ORDER):
        q = chip_of(d)
        for k in range(2):
            pout[q, k] = product(4 * q + 2 * (1 - core) + k)
        cp = remote(pout.at[q], pin.at[q], p_send.at[i], p_recv.at[q], r, pair)
        cp.start()
        sends.append(cp)
    for i, d in enumerate(Q_ORDER):
        q = chip_of(d)
        for k in range(2):
            sb[q, k] = product(4 * q + 2 * core + k)
        remote(pout.at[q], pin.at[q], p_send.at[i], p_recv.at[q], r, pair).wait_recv()
        for k in range(2):
            sb[q, k] = sb[q, k] + pin[q, k]
        if d != (0, 0):
            cp = remote(sb.at[q], rb.at[chip], s_send.at[i], s_recv.at[chip], r, q * 2 + core)
            cp.start()
            sends.append(cp)

    total = [sb[chip, 0], sb[chip, 1]]
    for d in Q_ORDER[:-1]:
        q = chip_of(d)
        remote(sb.at[q], rb.at[q], s_send.at[0], s_recv.at[q], r, c).wait_recv()
        for k in range(2):
            total[k] = total[k] + rb[q, k]
    contrib = []
    sq = jnp.zeros((NV, BS), F32)
    for k in range(2):
        res = rhs_v[k] - total[k]
        tmp[k] = res
        sq = sq + res * res
        hi, lo = split(res)
        whi, wlo = split(rest_v[k])
        o = lax.dot_general(
            jnp.concatenate([hi, lo], axis=0), jnp.concatenate([whi, wlo], axis=1),
            (((1,), (0,)), ((), ())), preferred_element_type=F32,
        )
        tmp[2 + k] = o[:NV, :BS] + (o[:NV, BS:] + o[NV:, :BS])
    resid_cp = pltpu.make_async_copy(tmp.at[pl.ds(0, 2)], resid_out, out_sem.at[0])
    resid_cp.start()

    lane = lax.broadcasted_iota(jnp.int32, (NV, BS), 1)
    sub = lax.broadcasted_iota(jnp.int32, (NV, BS), 0)
    eye = lane == sub
    sq_row = jnp.sum(jnp.where(eye, jnp.sum(sq, axis=1, keepdims=True), 0.0), axis=0, keepdims=True)
    for k in range(2):
        for v in range(2):
            aout[pl.ds(2 * k + v, NC, stride=8), :] = tmp[2 + k, pl.ds(v, NC, stride=2), :]
        aout[pl.ds(5 + k, NC, stride=8), :] = jnp.full((NC, BS), agg_s[k].astype(F32), F32)
    aout[pl.ds(4, NC, stride=8), :] = jnp.broadcast_to(sq_row, (NC, BS))
    aout[pl.ds(7, NC, stride=8), :] = jnp.zeros((NC, BS), F32)

    def tile(ref, j):
        return ref.at[pl.ds(pl.multiple_of(8 * j, 8), 8)]

    for d in range(1, NC):
        j = (c + d) % NC
        cp = remote(tile(aout, j), tile(ain, c), a_send.at[d], a_recv.at[c], r, j)
        cp.start()
        sends.append(cp)
    tile(ain, c)[...] = tile(aout, c)[...]

    who = lax.broadcasted_iota(jnp.int32, (NAGG, BS), 0).astype(F32)
    acc = [jnp.zeros((NAGG, BS), F32) for _ in range(2)]
    group_sq = jnp.zeros((1, BS), F32)
    for d in range(NC):
        j = (c + NC - d) % NC
        if d > 0:
            remote(tile(aout, j), tile(ain, j), a_send.at[0], a_recv.at[j], r, c).wait_recv()
        t = tile(ain, j)[...]
        for k in range(2):
            sel = who == t[5 + k:6 + k, :]
            for v in range(2):
                acc[v] = acc[v] + jnp.where(sel, t[2 * k + v:2 * k + v + 1, :], 0.0)
        group_sq = group_sq + t[4:5, :]
    tile(sqb, r)[...] = jnp.broadcast_to(group_sq, (8, BS))
    for d in range(1, NR):
        j = (r + d) % NR
        cp = remote(tile(sqb, r), tile(sqb, r), q_send.at[d], q_recv.at[r], j, c)
        cp.start()
        sends.append(cp)

    def slot(j):
        return cbuf.at[pl.ds(pl.multiple_of(16 * j, 16), 16)]

    slot(c)[0:8, :] = acc[0]
    slot(c)[8:16, :] = acc[1]
    for d in range(1, NC):
        j = (c + d) % NC
        cp = remote(slot(c), slot(c), b_send.at[d], b_recv.at[c], r, j)
        cp.start()
        sends.append(cp)

    all_sq = group_sq
    for d in range(1, NR):
        j = (r + NR - d) % NR
        remote(tile(sqb, j), tile(sqb, j), q_send.at[0], q_recv.at[j], r, c).wait_recv()
        all_sq = all_sq + tile(sqb, j)[0:1, :]
    mean = all_sq * (1.0 / (NR * GR * BS)) + 1e-6
    mean_v = jnp.sum(jnp.where(eye, jnp.broadcast_to(mean, (NV, BS)), 0.0), axis=1, keepdims=True)
    inv = jnp.broadcast_to(1.0 / jnp.sqrt(mean_v), (NV, BS))
    for d in range(1, NC):
        j = (c + NC - d) % NC
        remote(slot(j), slot(j), b_send.at[0], b_recv.at[j], r, c).wait_recv()
    for a in range(NAGG):
        ov[a] = cbuf[pl.ds(a, NV, stride=8), :] * inv
    coarse_out_cp = [
        pltpu.make_async_copy(ov, coarse_out, out_sem.at[1])
    ]
    for cp in sends:
        cp.wait_send()
    for cp in coarse_out_cp:
        cp.start()
    for cp in coarse_out_cp:
        cp.wait()
    resid_cp.wait()


def local(matrix, columns, counts, fine_guess, right_side, aggregate, restrict):
    dma = pltpu.SemaphoreType.DMA
    return pl.pallas_call(
        kernel,
        out_shape=(
            jax.ShapeDtypeStruct((NAGG, NV, BS), F32),
            jax.ShapeDtypeStruct((2, NV, BS), F32),
        ),
        in_specs=[pl.BlockSpec(memory_space=pl.ANY)] * 7,
        out_specs=(pl.BlockSpec(memory_space=pl.ANY),) * 2,
        scratch_shapes=[
            pltpu.VMEM((GR, KB, BS, BS), F32),
            pltpu.VMEM((GR, 2 * BS, KB * BS), BF16),
            pltpu.VMEM((2 * NR, NV, BS), F32),
            pltpu.VMEM((NQ, 2, NV, BS), F32),
            pltpu.VMEM((NQ, 2, NV, BS), F32),
            pltpu.VMEM((NQ, 2, NV, BS), F32),
            pltpu.VMEM((NQ, 2, NV, BS), F32),
            pltpu.VMEM((NC * 8, BS), F32),
            pltpu.VMEM((NC * 8, BS), F32),
            pltpu.VMEM((NC * 16, BS), F32),
            pltpu.VMEM((NR * 8, BS), F32),
            pltpu.VMEM((2, NV, BS), F32),
            pltpu.VMEM((2, BS, BS), F32),
            pltpu.VMEM((4, NV, BS), F32),
            pltpu.VMEM((NAGG, NV, BS), F32),
            pltpu.SMEM((GR, KB), jnp.int32),
            pltpu.SMEM((GR, 1), jnp.int32),
            pltpu.SMEM((2,), jnp.int32),
            dma((CHUNKS,)), dma((6,)),
            dma((16,)), dma((NR,)),
            dma((NQ,)), dma((NQ,)),
            dma((NQ,)), dma((NQ,)),
            dma((NC,)), dma((NC,)),
            dma((NC,)), dma((NC,)),
            dma((NR,)), dma((NR,)),
            dma((2,)),
        ],
        compiler_params=pltpu.CompilerParams(collective_id=0, has_side_effects=True),
    )(matrix, columns, counts, fine_guess, right_side, aggregate, restrict)


def solution(mesh):
    in_specs = (
        P("row", "col", None, None),
        P("row", "col"),
        P("row", "col"),
        P(("col", "row"), None, None),
        P(("row", "col"), None, None),
        P(("row", "col")),
        P(("row", "col"), None, None),
    )
    out_specs = (P("row", None, None), P(("row", "col"), None, None))
    return jax.shard_map(local, mesh=mesh, in_specs=in_specs, out_specs=out_specs, check_vma=False)
```

time: 103 us -> 49.3 us (0.48)
  blocking collectives: 52.9 us -> 0 us
  Pallas kernels: 0 us -> 42.8 us
  waiting for transfers between devices: 20.5 us -> 0 us
  starting transfers between devices: 13.5 us -> 0 us
  matrix products: 6.73 us -> 0 us
  other arithmetic: 4.35 us -> 0 us
  local copies, waits for them, and re-layouts: 4.33 us -> 5.65 us
    all_to_all x2 -> x0, blocking collectives: 52.9 us -> none  [the longest x1 32.7 us: sent_to_all(): lax.all_to_all(jnp.broadcast_to(x[None], (length, *x.shape)), axis, 0, 0,...]
    pallas_call x0 -> x1, Pallas kernels: none -> 42.8 us  [local(): pl.pallas_call(kernel, out_shape=(jax.ShapeDtypeStruct((NAGG, NV, BS), F3...]
    all_to_all x2 -> x0, waiting for transfers between devices: 20.5 us -> none  [sent_to_all(): lax.all_to_all(jnp.broadcast_to(x[None], (length, *x.shape)), axis, 0, 0,...]
    all_to_all x2 -> x0, starting transfers between devices: 13.5 us -> none  [sent_to_all(): lax.all_to_all(jnp.broadcast_to(x[None], (length, *x.shape)), axis, 0, 0,...]
    dot_general x3 -> x0, matrix products: 6.73 us -> none  [the longest x1 6.2 us: local(): jnp.einsum('gsab,gsvb->gva', matrix, picked, precision=lax.Precision.HIGH...]
    unnamed x8 -> x4, local copies, waits for them, and re-layouts: 0.03 us -> 5.65 us
    broadcast_in_dim x4 -> x0, local copies, waits for them, and re-layouts: 3.43 us -> none  [the longest x3 3.33 us: sent_to_all(): jnp.broadcast_to(x[None], (length, *x.shape))]
    reduce_sum x4 -> x0, other arithmetic: 1.48 us -> none  [the longest x2 1.33 us: over_copies(): return jnp.sum(everything, axis=0)]
  transfers between devices with their start and end apart: 2 -> 0, of which waited for: 2 -> 0; matrix products, arithmetic and copies ran while one was open for 2% -> 0% of each run, Pallas kernels for 0% -> 0%
where the time goes in v1:
time: 49.3 us; the launch traced here: 49.1 us
  Pallas kernels  42.8 us (87%)
  local copies, waits for them, and re-layouts  5.65 us (11%)
  between operations  0.64 us (1%)
    pallas_call x1, Pallas kernels, local(): pl.pallas_call(kernel, out_shape=(jax.ShapeDtypeStruct((NAGG, NV, BS), F3...  42.8 us
    unnamed x4, local copies, waits for them, and re-layouts  5.65 us

profile of v1, /device:TPU:1, one launch (start us, length us, event | category | flops | bytes accessed | tf_op | source)
XLA Modules:
  0.0 49.1 jit_solution(8695894220845174451)
XLA Ops:
  0.6 1.4 %copy.9.cols = s32[32,2]{1,0:T(8,128)} copy(s32[32,2]{0,1:T(2,128)} %param.8) | data formatting | bytes 512 | tf_op args[1]
  2.0 1.3 %copy.10.cnts = s32[32,1]{1,0:T(8,128)} copy(s32[32,1]{0,1:T(1,128)} %param.9) | data formatting | bytes 256 | tf_op args[2]
  3.3 42.8 %shard_map.86 = (f32[8,32,128]{2,1,0:T(8,128)}, f32[2,32,128]{2,1,0:T(8,128)}) custom-call(f32[32,2,128,128]{3,2,1,0:T(8,128)} %mat.1, s32[32,2]{1,0:T(8,128)} %copy.9.cols, s32[32,1]{1,0:T(8,128)} %copy.10.cnts, f32[2,32,128]{2,1,0:T(8,128)} %xin.1, f32[2,32,128]{2,1,0:T(8,128)} %rhs.1, s32[2]{0:T(128)} %agg.1, f32[2,128,128]{2,1,0:T(8,128)} %rest.1), custom_call_target="tpu_custom_call" | custom-call | tf_op jit(solution)/shard_map/pallas_call | solution.py:248
  46.1 1.6 %copy.13 = f32[8,32,128]{2,1,0:T(8,128)} copy(f32[8,32,128]{2,1,0:T(8,128)} %get-tuple-element.4) | data formatting | bytes 262144
  47.7 1.4 %copy.14 = f32[2,32,128]{2,1,0:T(8,128)} copy(f32[2,32,128]{2,1,0:T(8,128)} %get-tuple-element.5) | data formatting | bytes 65536

commit v2 on v1

--- a/solution.py
+++ b/solution.py
@@ -24,12 +24,17 @@
     return hi, (x - hi.astype(F32)).astype(BF16)
 
 
+def diagonal():
+    lane = lax.broadcasted_iota(jnp.int32, (NV, BS), 1)
+    return lane == lax.broadcasted_iota(jnp.int32, (NV, BS), 0)
+
+
 def kernel(
-    mat, cols, cnts, xin, rhs, agg, rest, coarse_out, resid_out,
-    mraw, mw, xg, pout, pin, sb, rb, aout, ain, cbuf, sqb, rhs_v, rest_v, tmp, ov,
+    mat, cols, cnts, xin, rhs, agg, rest, cbuf, sqb, resid,
+    mraw, mw, xg, pout, pin, sb, rb, aout, ain, rhs_v, rest_v, tmp,
     cols_s, cnts_s, agg_s,
     mat_sem, loc_sem, ag_send, ag_recv, p_send, p_recv, s_send, s_recv,
-    a_send, a_recv, b_send, b_recv, q_send, q_recv, out_sem,
+    a_send, a_recv, b_send, b_recv, q_send, q_recv,
 ):
     r = lax.axis_index("row")
     c = lax.axis_index("col")
@@ -43,6 +48,7 @@
             device_id=(row, col), device_id_type=MESH,
         )
 
+    sends = []
     own_x = pltpu.make_async_copy(xin, xg.at[pl.ds(2 * r, 2)], loc_sem.at[0])
     own_x.start()
     per = GR // CHUNKS
@@ -79,7 +85,6 @@
         ref = xg.at[pl.ds(2 * block_row, 2)]
         return remote(ref, ref, ag_send.at[s], ag_recv.at[block_row], to_row, c)
 
-    sends = []
     for i, d in enumerate(Z_ORDER):
         cp = ag(r, ((z + d) % NZ) * 2 + xl, i)
         cp.start()
@@ -112,8 +117,8 @@
         ag(((z + NZ - d) % NZ) * 2 + 1 - xl, r, 0).wait_recv()
 
     def product(g):
-        used = jnp.where(cnts_s[g, 0] > 1, 1.0, 0.0).astype(F32)
-        x = jnp.concatenate([xg[cols_s[g, 0]], xg[cols_s[g, 1]] * used], axis=1)
+        used = jnp.where(cnts_s[0, g] > 1, 1.0, 0.0).astype(F32)
+        x = jnp.concatenate([xg[cols_s[0, g]], xg[cols_s[1, g]] * used], axis=1)
         hi, lo = split(x)
         o = lax.dot_general(
             jnp.concatenate([hi, lo], axis=0), mw[g], (((1,), (1,)), ((), ())),
@@ -154,7 +159,7 @@
     sq = jnp.zeros((NV, BS), F32)
     for k in range(2):
         res = rhs_v[k] - total[k]
-        tmp[k] = res
+        resid[k] = res
         sq = sq + res * res
         hi, lo = split(res)
         whi, wlo = split(rest_v[k])
@@ -162,17 +167,13 @@
             jnp.concatenate([hi, lo], axis=0), jnp.concatenate([whi, wlo], axis=1),
             (((1,), (0,)), ((), ())), preferred_element_type=F32,
         )
-        tmp[2 + k] = o[:NV, :BS] + (o[:NV, BS:] + o[NV:, :BS])
-    resid_cp = pltpu.make_async_copy(tmp.at[pl.ds(0, 2)], resid_out, out_sem.at[0])
-    resid_cp.start()
-
-    lane = lax.broadcasted_iota(jnp.int32, (NV, BS), 1)
-    sub = lax.broadcasted_iota(jnp.int32, (NV, BS), 0)
-    eye = lane == sub
+        tmp[k] = o[:NV, :BS] + (o[:NV, BS:] + o[NV:, :BS])
+
+    eye = diagonal()
     sq_row = jnp.sum(jnp.where(eye, jnp.sum(sq, axis=1, keepdims=True), 0.0), axis=0, keepdims=True)
     for k in range(2):
         for v in range(2):
-            aout[pl.ds(2 * k + v, NC, stride=8), :] = tmp[2 + k, pl.ds(v, NC, stride=2), :]
+            aout[pl.ds(2 * k + v, NC, stride=8), :] = tmp[k, pl.ds(v, NC, stride=2), :]
         aout[pl.ds(5 + k, NC, stride=8), :] = jnp.full((NC, BS), agg_s[k].astype(F32), F32)
     aout[pl.ds(4, NC, stride=8), :] = jnp.broadcast_to(sq_row, (NC, BS))
     aout[pl.ds(7, NC, stride=8), :] = jnp.zeros((NC, BS), F32)
@@ -218,41 +219,38 @@
         cp.start()
         sends.append(cp)
 
-    all_sq = group_sq
     for d in range(1, NR):
         j = (r + NR - d) % NR
         remote(tile(sqb, j), tile(sqb, j), q_send.at[0], q_recv.at[j], r, c).wait_recv()
-        all_sq = all_sq + tile(sqb, j)[0:1, :]
-    mean = all_sq * (1.0 / (NR * GR * BS)) + 1e-6
-    mean_v = jnp.sum(jnp.where(eye, jnp.broadcast_to(mean, (NV, BS)), 0.0), axis=1, keepdims=True)
-    inv = jnp.broadcast_to(1.0 / jnp.sqrt(mean_v), (NV, BS))
     for d in range(1, NC):
         j = (c + NC - d) % NC
         remote(slot(j), slot(j), b_send.at[0], b_recv.at[j], r, c).wait_recv()
-    for a in range(NAGG):
-        ov[a] = cbuf[pl.ds(a, NV, stride=8), :] * inv
-    coarse_out_cp = [
-        pltpu.make_async_copy(ov, coarse_out, out_sem.at[1])
-    ]
     for cp in sends:
         cp.wait_send()
-    for cp in coarse_out_cp:
-        cp.start()
-    for cp in coarse_out_cp:
-        cp.wait()
-    resid_cp.wait()
+
+
+def finish(cbuf, sqb, resid, coarse_out, resid_out):
+    all_sq = jnp.sum(sqb[...], axis=0, keepdims=True) * 0.125
+    mean = all_sq * (1.0 / (NR * GR * BS)) + 1e-6
+    mean_v = jnp.sum(jnp.where(diagonal(), jnp.broadcast_to(mean, (NV, BS)), 0.0), axis=1, keepdims=True)
+    inv = jnp.broadcast_to(1.0 / jnp.sqrt(mean_v), (NV, BS))
+    for a in range(NAGG):
+        coarse_out[a] = cbuf[pl.ds(a, NV, stride=8), :] * inv
+    resid_out[...] = resid[...]
 
 
 def local(matrix, columns, counts, fine_guess, right_side, aggregate, restrict):
     dma = pltpu.SemaphoreType.DMA
-    return pl.pallas_call(
+    vmem = pl.BlockSpec(memory_space=pltpu.VMEM)
+    parts = pl.pallas_call(
         kernel,
         out_shape=(
-            jax.ShapeDtypeStruct((NAGG, NV, BS), F32),
-            jax.ShapeDtypeStruct((2, NV, BS), F32),
+            pltpu.VMEM((NC * 16, BS), F32),
+            pltpu.VMEM((NR * 8, BS), F32),
+            pltpu.VMEM((2, NV, BS), F32),
         ),
-        in_specs=[pl.BlockSpec(memory_space=pl.ANY)] * 7,
-        out_specs=(pl.BlockSpec(memory_space=pl.ANY),) * 2,
+        in_specs=[pl.BlockSpec(memory_space=pltpu.HBM)] * 7,
+        out_specs=(vmem,) * 3,
         scratch_shapes=[
             pltpu.VMEM((GR, KB, BS, BS), F32),
             pltpu.VMEM((GR, 2 * BS, KB * BS), BF16),
@@ -263,14 +261,11 @@
             pltpu.VMEM((NQ, 2, NV, BS), F32),
             pltpu.VMEM((NC * 8, BS), F32),
             pltpu.VMEM((NC * 8, BS), F32),
-            pltpu.VMEM((NC * 16, BS), F32),
-            pltpu.VMEM((NR * 8, BS), F32),
             pltpu.VMEM((2, NV, BS), F32),
             pltpu.VMEM((2, BS, BS), F32),
-            pltpu.VMEM((4, NV, BS), F32),
-            pltpu.VMEM((NAGG, NV, BS), F32),
-            pltpu.SMEM((GR, KB), jnp.int32),
-            pltpu.SMEM((GR, 1), jnp.int32),
+            pltpu.VMEM((2, NV, BS), F32),
+            pltpu.SMEM((KB, GR), jnp.int32),
+            pltpu.SMEM((1, GR), jnp.int32),
             pltpu.SMEM((2,), jnp.int32),
             dma((CHUNKS,)), dma((6,)),
             dma((16,)), dma((NR,)),
@@ -279,10 +274,19 @@
             dma((NC,)), dma((NC,)),
             dma((NC,)), dma((NC,)),
             dma((NR,)), dma((NR,)),
-            dma((2,)),
         ],
-        compiler_params=pltpu.CompilerParams(collective_id=0, has_side_effects=True),
-    )(matrix, columns, counts, fine_guess, right_side, aggregate, restrict)
+        compiler_params=pltpu.CompilerParams(collective_id=0, has_side_effects=True, vmem_limit_bytes=60 * 2**20),
+    )(matrix, columns.T, counts.T, fine_guess, right_side, aggregate, restrict)
+    return pl.pallas_call(
+        finish,
+        out_shape=(
+            jax.ShapeDtypeStruct((NAGG, NV, BS), F32),
+            jax.ShapeDtypeStruct((2, NV, BS), F32),
+        ),
+        in_specs=[vmem] * 3,
+        out_specs=(vmem,) * 2,
+        compiler_params=pltpu.CompilerParams(vmem_limit_bytes=4 * 2**20),
+    )(*parts)
 
 
 def solution(mesh):

time: 49.3 us -> 43.8 us (0.89)
  local copies, waits for them, and re-layouts: 5.65 us -> 0 us
    unnamed x4 -> x0, local copies, waits for them, and re-layouts: 5.65 us -> none
    pallas_call x1 -> x2, Pallas kernels: 42.8 us -> 43.1 us  [the longest x1 42.3 us: local(): pl.pallas_call(kernel, out_shape=(pltpu.VMEM((NC * 16, BS), F32), pltpu.V...]
where the time goes in v2:
time: 43.8 us; the launch traced here: 43.7 us
  Pallas kernels  43.1 us (98%)
  between operations  0.64 us (1%)
    pallas_call x1, Pallas kernels, local(): pl.pallas_call(kernel, out_shape=(pltpu.VMEM((NC * 16, BS), F32), pltpu.V...  42.3 us

profile of v2, /device:TPU:1, one launch (start us, length us, event | category | flops | bytes accessed | tf_op | source)
XLA Modules:
  0.0 43.7 jit_solution(7800532842298923710)
XLA Ops:
  0.6 42.3 %shard_map.86 = (f32[256,128]{1,0:T(8,128)S(1)}, f32[128,128]{1,0:T(8,128)S(1)}, f32[2,32,128]{2,1,0:T(8,128)S(1)}) custom-call(f32[32,2,128,128]{3,2,1,0:T(8,128)} %mat.1, s32[2,32]{1,0:T(2,128)} %bitcast.2, s32[1,32]{1,0:T(1,128)} %bitcast.3, f32[2,32,128]{2,1,0:T(8,128)} %xin.1, f32[2,32,128]{2,1,0:T(8,128)} %rhs.1, s32[2]{0:T(128)} %agg.1, ...), custom_call_target="tpu_custom_call" | custom-call | tf_op jit(solution)/shard_map/pallas_call | solution.py:245
  43.0 0.8 %shard_map.87 = (f32[8,32,128]{2,1,0:T(8,128)}, f32[2,32,128]{2,1,0:T(8,128)}) custom-call(f32[256,128]{1,0:T(8,128)S(1)} %get-tuple-element.5.cbuf, f32[128,128]{1,0:T(8,128)S(1)} %get-tuple-element.6.sqb, f32[2,32,128]{2,1,0:T(8,128)S(1)} %get-tuple-element.7.resid), custom_call_target="tpu_custom_call" | custom-call | tf_op jit(solution)/shard_map/pallas_call | solution.py:280

commit v3 on v2

--- a/solution.py
+++ b/solution.py
@@ -15,7 +15,6 @@
 GR, KB, NV, BS = 32, 2, 32, 128
 NAGG = 8
 CHUNKS = 4
-Z_ORDER = (4, 3, 5, 2, 6, 1, 7)
 Q_ORDER = ((2, 1), (1, 1), (3, 1), (2, 0), (0, 1), (1, 0), (3, 0), (0, 0))
 
 
@@ -31,10 +30,10 @@
 
 def kernel(
     mat, cols, cnts, xin, rhs, agg, rest, cbuf, sqb, resid,
-    mraw, mw, xg, pout, pin, sb, rb, aout, ain, rhs_v, rest_v, tmp,
+    mraw, mw, xg, pout, pin, sb, rb, aout, ain, rhs_v, rest_v, rw, tmp, sqs, sqa,
     cols_s, cnts_s, agg_s,
     mat_sem, loc_sem, ag_send, ag_recv, p_send, p_recv, s_send, s_recv,
-    a_send, a_recv, b_send, b_recv, q_send, q_recv,
+    a_send, a_recv, b_send, b_recv, o_send, o_recv, q_send, q_recv, tok,
 ):
     r = lax.axis_index("row")
     c = lax.axis_index("col")
@@ -70,28 +69,60 @@
 
     barrier = pltpu.get_barrier_semaphore()
 
-    def greet(d, carry):
-        pl.semaphore_signal(barrier, inc=1, device_id=((r + d) % NR, c), device_id_type=MESH)
-        pl.semaphore_signal(barrier, inc=1, device_id=(r, (c + d) % NC), device_id_type=MESH)
-        return carry
-
-    lax.fori_loop(1, 16, greet, 0)
+    def z_row(d):
+        return ((z + NZ + d) % NZ) * 2 + xl
+
+    def chip_of(dy, dx):
+        return ((y + dy) % 4) * 2 + (xh + dx) % 2
+
+    def col_of(dy, dx):
+        return chip_of(dy, dx) * 2 + core
+
+    other = z * 2 + 1 - xl
+    pair = chip * 2 + 1 - core
+    near = [(z_row(d), c) for d in (2, -2, 1, -1)]
+    near += [(other, c), (r, col_of(0, 1)), (r, col_of(1, 0)), (r, col_of(3, 0)), (r, pair)]
+    for dev in near:
+        pl.semaphore_signal(barrier, inc=1, device_id=dev, device_id_type=MESH)
     own_x.wait()
-    pl.semaphore_wait(barrier, NR - 1 + NC - 1)
-
-    other = z * 2 + 1 - xl
-
-    def ag(block_row, to_row, s):
-        ref = xg.at[pl.ds(2 * block_row, 2)]
-        return remote(ref, ref, ag_send.at[s], ag_recv.at[block_row], to_row, c)
-
-    for i, d in enumerate(Z_ORDER):
-        cp = ag(r, ((z + d) % NZ) * 2 + xl, i)
-        cp.start()
-        sends.append(cp)
-    cp = ag(r, other, 7)
-    cp.start()
-    sends.append(cp)
+    pl.semaphore_wait(barrier, len(near))
+
+    def ag(row, half, to_row):
+        if half is None:
+            ref, sem = xg.at[pl.ds(2 * row, 2)], 2 * row
+        else:
+            ref, sem = xg.at[pl.ds(2 * row + half, 1)], 2 * row + half
+        return remote(ref, ref, ag_send.at[len(sends)], ag_recv.at[sem], to_row, c)
+
+    def pass_on(row, half, *targets):
+        for to_row in targets:
+            cp = ag(row, half, to_row)
+            cp.start()
+            sends.append(cp)
+
+    def arrived(row, half=None):
+        ag(row, half, r).wait_recv()
+
+    def across(d):
+        return ((z + NZ + d) % NZ) * 2 + 1 - xl
+
+    pass_on(r, None, other, z_row(2), z_row(-2), z_row(1), z_row(-1))
+    for dy in (1, 3):
+        pl.semaphore_signal(tok.at[0], inc=1, device_id=(r, col_of(dy, 0)), device_id_type=MESH)
+    arrived(other)
+    pass_on(other, None, z_row(1), z_row(-1))
+    for s in (1, -1):
+        arrived(z_row(-2 * s))
+        pass_on(z_row(-2 * s), None, other, z_row(s))
+        pass_on(z_row(-2 * s), (1 - s) // 2, z_row(2 * s))
+    pl.semaphore_wait(tok.at[0], 2)
+    pl.semaphore_signal(tok.at[1], inc=1, device_id=(r, col_of(0, 1)), device_id_type=MESH)
+    for s in (1, -1):
+        arrived(z_row(-3 * s))
+        pass_on(z_row(-3 * s), None, other)
+    for half in (0, 1):
+        arrived(z_row(4), half)
+        pass_on(z_row(4), half, other)
 
     for k in range(CHUNKS):
         mats[k].wait()
@@ -104,17 +135,21 @@
             return carry
 
         lax.fori_loop(k * per, (k + 1) * per, parts, 0)
-
-    for i, d in enumerate(Z_ORDER):
-        zr = ((z + NZ - d) % NZ) * 2 + xl
-        ag(zr, r, 0).wait_recv()
-        cp = ag(zr, other, 8 + i)
-        cp.start()
-        sends.append(cp)
     for m in smalls:
         m.wait()
-    for d in (0,) + Z_ORDER:
-        ag(((z + NZ - d) % NZ) * 2 + 1 - xl, r, 0).wait_recv()
+    for k in range(2):
+        whi, wlo = split(rest_v[k])
+        rw[k, :, 0:BS] = whi
+        rw[k, :, BS:2 * BS] = wlo
+    for s in (1, -1):
+        arrived(z_row(s))
+        arrived(across(s))
+        arrived(across(2 * s))
+    for s in (1, -1):
+        arrived(across(3 * s))
+    for half in (0, 1):
+        arrived(across(4), half)
+    pl.semaphore_wait(tok.at[1], 1)
 
     def product(g):
         used = jnp.where(cnts_s[0, g] > 1, 1.0, 0.0).astype(F32)
@@ -126,19 +161,15 @@
         )
         return o[:NV, :BS] + (o[:NV, BS:] + o[NV:, :BS])
 
-    def chip_of(d):
-        return ((y + d[0]) % 4) * 2 + (xh + d[1]) % 2
-
-    pair = chip * 2 + 1 - core
     for i, d in enumerate(Q_ORDER):
-        q = chip_of(d)
+        q = chip_of(*d)
         for k in range(2):
             pout[q, k] = product(4 * q + 2 * (1 - core) + k)
         cp = remote(pout.at[q], pin.at[q], p_send.at[i], p_recv.at[q], r, pair)
         cp.start()
         sends.append(cp)
     for i, d in enumerate(Q_ORDER):
-        q = chip_of(d)
+        q = chip_of(*d)
         for k in range(2):
             sb[q, k] = product(4 * q + 2 * core + k)
         remote(pout.at[q], pin.at[q], p_send.at[i], p_recv.at[q], r, pair).wait_recv()
@@ -151,7 +182,7 @@
 
     total = [sb[chip, 0], sb[chip, 1]]
     for d in Q_ORDER[:-1]:
-        q = chip_of(d)
+        q = chip_of(*d)
         remote(sb.at[q], rb.at[q], s_send.at[0], s_recv.at[q], r, c).wait_recv()
         for k in range(2):
             total[k] = total[k] + rb[q, k]
@@ -162,9 +193,8 @@
         resid[k] = res
         sq = sq + res * res
         hi, lo = split(res)
-        whi, wlo = split(rest_v[k])
         o = lax.dot_general(
-            jnp.concatenate([hi, lo], axis=0), jnp.concatenate([whi, wlo], axis=1),
+            jnp.concatenate([hi, lo], axis=0), rw[k],
             (((1,), (0,)), ((), ())), preferred_element_type=F32,
         )
         tmp[k] = o[:NV, :BS] + (o[:NV, BS:] + o[NV:, :BS])
@@ -178,12 +208,21 @@
     aout[pl.ds(4, NC, stride=8), :] = jnp.broadcast_to(sq_row, (NC, BS))
     aout[pl.ds(7, NC, stride=8), :] = jnp.zeros((NC, BS), F32)
 
+    sqs[...] = jnp.broadcast_to(sq_row, (8, BS))
+
+    def line(ref, j):
+        return ref.at[pl.ds(pl.multiple_of(8 * j, 8), 1)]
+
     def tile(ref, j):
         return ref.at[pl.ds(pl.multiple_of(8 * j, 8), 8)]
 
     for d in range(1, NC):
         j = (c + d) % NC
         cp = remote(tile(aout, j), tile(ain, c), a_send.at[d], a_recv.at[c], r, j)
+        cp.start()
+        sends.append(cp)
+    for d in range(NC):
+        cp = remote(line(sqs, 0), line(sqa, c), o_send.at[d], o_recv.at[c], other, (c + d) % NC)
         cp.start()
         sends.append(cp)
     tile(ain, c)[...] = tile(aout, c)[...]
@@ -201,12 +240,6 @@
             for v in range(2):
                 acc[v] = acc[v] + jnp.where(sel, t[2 * k + v:2 * k + v + 1, :], 0.0)
         group_sq = group_sq + t[4:5, :]
-    tile(sqb, r)[...] = jnp.broadcast_to(group_sq, (8, BS))
-    for d in range(1, NR):
-        j = (r + d) % NR
-        cp = remote(tile(sqb, r), tile(sqb, r), q_send.at[d], q_recv.at[r], j, c)
-        cp.start()
-        sends.append(cp)
 
     def slot(j):
         return cbuf.at[pl.ds(pl.multiple_of(16 * j, 16), 16)]
@@ -219,9 +252,20 @@
         cp.start()
         sends.append(cp)
 
-    for d in range(1, NR):
-        j = (r + NR - d) % NR
-        remote(tile(sqb, j), tile(sqb, j), q_send.at[0], q_recv.at[j], r, c).wait_recv()
+    plane_sq = group_sq
+    for d in range(NC):
+        j = (c + NC - d) % NC
+        remote(line(sqs, 0), line(sqa, j), o_send.at[0], o_recv.at[j], r, c).wait_recv()
+        plane_sq = plane_sq + line(sqa, j)[...]
+    tile(sqb, z)[...] = jnp.broadcast_to(plane_sq, (8, BS))
+    for d in (4, 3, 5, 2, 6, 1, 7):
+        cp = remote(line(sqb, z), line(sqb, z), q_send.at[d], q_recv.at[z], z_row(d), c)
+        cp.start()
+        sends.append(cp)
+
+    for d in range(1, NZ):
+        j = (z + d) % NZ
+        remote(line(sqb, j), line(sqb, j), q_send.at[0], q_recv.at[j], r, c).wait_recv()
     for d in range(1, NC):
         j = (c + NC - d) % NC
         remote(slot(j), slot(j), b_send.at[0], b_recv.at[j], r, c).wait_recv()
@@ -230,7 +274,7 @@
 
 
 def finish(cbuf, sqb, resid, coarse_out, resid_out):
-    all_sq = jnp.sum(sqb[...], axis=0, keepdims=True) * 0.125
+    all_sq = jnp.sum(sqb[pl.ds(0, NZ, stride=8), :], axis=0, keepdims=True)
     mean = all_sq * (1.0 / (NR * GR * BS)) + 1e-6
     mean_v = jnp.sum(jnp.where(diagonal(), jnp.broadcast_to(mean, (NV, BS)), 0.0), axis=1, keepdims=True)
     inv = jnp.broadcast_to(1.0 / jnp.sqrt(mean_v), (NV, BS))
@@ -246,7 +290,7 @@
         kernel,
         out_shape=(
             pltpu.VMEM((NC * 16, BS), F32),
-            pltpu.VMEM((NR * 8, BS), F32),
+            pltpu.VMEM((NZ * 8, BS), F32),
             pltpu.VMEM((2, NV, BS), F32),
         ),
         in_specs=[pl.BlockSpec(memory_space=pltpu.HBM)] * 7,
@@ -263,17 +307,22 @@
             pltpu.VMEM((NC * 8, BS), F32),
             pltpu.VMEM((2, NV, BS), F32),
             pltpu.VMEM((2, BS, BS), F32),
+            pltpu.VMEM((2, BS, 2 * BS), BF16),
             pltpu.VMEM((2, NV, BS), F32),
+            pltpu.VMEM((8, BS), F32),
+            pltpu.VMEM((NC * 8, BS), F32),
             pltpu.SMEM((KB, GR), jnp.int32),
             pltpu.SMEM((1, GR), jnp.int32),
             pltpu.SMEM((2,), jnp.int32),
             dma((CHUNKS,)), dma((6,)),
-            dma((16,)), dma((NR,)),
+            dma((24,)), dma((2 * NR,)),
             dma((NQ,)), dma((NQ,)),
             dma((NQ,)), dma((NQ,)),
             dma((NC,)), dma((NC,)),
             dma((NC,)), dma((NC,)),
-            dma((NR,)), dma((NR,)),
+            dma((NC,)), dma((NC,)),
+            dma((NZ,)), dma((NZ,)),
+            pltpu.SemaphoreType.REGULAR((2,)),
         ],
         compiler_params=pltpu.CompilerParams(collective_id=0, has_side_effects=True, vmem_limit_bytes=60 * 2**20),
     )(matrix, columns.T, counts.T, fine_guess, right_side, aggregate, restrict)

time: 43.8 us -> 41.5 us (0.947)
  Pallas kernels: 43.1 us -> 40.8 us
    pallas_call x1, Pallas kernels: 42.3 us -> 40 us  [local(): pl.pallas_call(kernel, out_shape=(pltpu.VMEM((NC * 16, BS), F32), pltpu.V...]
where the time goes in v3:
time: 41.5 us; the launch traced here: 41.4 us
  Pallas kernels  40.8 us (98%)
  between operations  0.64 us (2%)
    pallas_call x1, Pallas kernels, local(): pl.pallas_call(kernel, out_shape=(pltpu.VMEM((NC * 16, BS), F32), pltpu.V...  40 us

profile of v3, /device:TPU:1, one launch (start us, length us, event | category | flops | bytes accessed | tf_op | source)
XLA Modules:
  0.0 41.4 jit_solution(16219876369052316364)
XLA Ops:
  0.6 40.0 %shard_map.86 = (f32[256,128]{1,0:T(8,128)S(1)}, f32[64,128]{1,0:T(8,128)S(1)}, f32[2,32,128]{2,1,0:T(8,128)S(1)}) custom-call(f32[32,2,128,128]{3,2,1,0:T(8,128)} %mat.1, s32[2,32]{1,0:T(2,128)} %bitcast.2, s32[1,32]{1,0:T(1,128)} %bitcast.3, f32[2,32,128]{2,1,0:T(8,128)} %xin.1, f32[2,32,128]{2,1,0:T(8,128)} %rhs.1, s32[2]{0:T(128)} %agg.1, ...), custom_call_target="tpu_custom_call" | custom-call | tf_op jit(solution)/shard_map/pallas_call | solution.py:289
  40.6 0.8 %shard_map.87 = (f32[8,32,128]{2,1,0:T(8,128)}, f32[2,32,128]{2,1,0:T(8,128)}) custom-call(f32[256,128]{1,0:T(8,128)S(1)} %get-tuple-element.5.cbuf, f32[64,128]{1,0:T(8,128)S(1)} %get-tuple-element.6.sqb, f32[2,32,128]{2,1,0:T(8,128)S(1)} %get-tuple-element.7.resid), custom_call_target="tpu_custom_call" | custom-call | tf_op jit(solution)/shard_map/pallas_call | solution.py:329

commit v4 on v3

--- a/solution.py
+++ b/solution.py
@@ -48,6 +48,23 @@
         )
 
     sends = []
+    barrier = pltpu.get_barrier_semaphore()
+
+    def z_row(d):
+        return ((z + NZ + d) % NZ) * 2 + xl
+
+    def chip_of(dy, dx):
+        return ((y + dy) % 4) * 2 + (xh + dx) % 2
+
+    def col_of(dy, dx):
+        return chip_of(dy, dx) * 2 + core
+
+    other = z * 2 + 1 - xl
+    pair = chip * 2 + 1 - core
+    near = [(z_row(d), c) for d in (2, -2, 1, -1)]
+    near += [(other, c), (r, col_of(0, 1)), (r, col_of(1, 0)), (r, col_of(3, 0)), (r, pair)]
+    for dev in near:
+        pl.semaphore_signal(barrier, inc=1, device_id=dev, device_id_type=MESH)
     own_x = pltpu.make_async_copy(xin, xg.at[pl.ds(2 * r, 2)], loc_sem.at[0])
     own_x.start()
     per = GR // CHUNKS
@@ -67,23 +84,6 @@
     for m in smalls:
         m.start()
 
-    barrier = pltpu.get_barrier_semaphore()
-
-    def z_row(d):
-        return ((z + NZ + d) % NZ) * 2 + xl
-
-    def chip_of(dy, dx):
-        return ((y + dy) % 4) * 2 + (xh + dx) % 2
-
-    def col_of(dy, dx):
-        return chip_of(dy, dx) * 2 + core
-
-    other = z * 2 + 1 - xl
-    pair = chip * 2 + 1 - core
-    near = [(z_row(d), c) for d in (2, -2, 1, -1)]
-    near += [(other, c), (r, col_of(0, 1)), (r, col_of(1, 0)), (r, col_of(3, 0)), (r, pair)]
-    for dev in near:
-        pl.semaphore_signal(barrier, inc=1, device_id=dev, device_id_type=MESH)
     own_x.wait()
     pl.semaphore_wait(barrier, len(near))
 
@@ -107,22 +107,20 @@
         return ((z + NZ + d) % NZ) * 2 + 1 - xl
 
     pass_on(r, None, other, z_row(2), z_row(-2), z_row(1), z_row(-1))
+    for d in (2, -2, 1, -1):
+        pl.semaphore_signal(tok.at[2], inc=1, device_id=(z_row(d), c), device_id_type=MESH)
     for dy in (1, 3):
         pl.semaphore_signal(tok.at[0], inc=1, device_id=(r, col_of(dy, 0)), device_id_type=MESH)
     arrived(other)
     pass_on(other, None, z_row(1), z_row(-1))
+    pl.semaphore_wait(tok.at[2], 4)
     for s in (1, -1):
-        arrived(z_row(-2 * s))
-        pass_on(z_row(-2 * s), None, other, z_row(s))
-        pass_on(z_row(-2 * s), (1 - s) // 2, z_row(2 * s))
+        far = z_row(-2 * s)
+        arrived(far)
+        pass_on(far, (1 - s) // 2, across(2 * s), z_row(2 * s))
+        pass_on(far, None, across(s), z_row(s), other)
     pl.semaphore_wait(tok.at[0], 2)
     pl.semaphore_signal(tok.at[1], inc=1, device_id=(r, col_of(0, 1)), device_id_type=MESH)
-    for s in (1, -1):
-        arrived(z_row(-3 * s))
-        pass_on(z_row(-3 * s), None, other)
-    for half in (0, 1):
-        arrived(z_row(4), half)
-        pass_on(z_row(4), half, other)
 
     for k in range(CHUNKS):
         mats[k].wait()
@@ -145,9 +143,10 @@
         arrived(z_row(s))
         arrived(across(s))
         arrived(across(2 * s))
-    for s in (1, -1):
+        arrived(z_row(3 * s))
         arrived(across(3 * s))
     for half in (0, 1):
+        arrived(z_row(4), half)
         arrived(across(4), half)
     pl.semaphore_wait(tok.at[1], 1)
 
@@ -322,7 +321,7 @@
             dma((NC,)), dma((NC,)),
             dma((NC,)), dma((NC,)),
             dma((NZ,)), dma((NZ,)),
-            pltpu.SemaphoreType.REGULAR((2,)),
+            pltpu.SemaphoreType.REGULAR((3,)),
         ],
         compiler_params=pltpu.CompilerParams(collective_id=0, has_side_effects=True, vmem_limit_bytes=60 * 2**20),
     )(matrix, columns.T, counts.T, fine_guess, right_side, aggregate, restrict)

time: 41.5 us -> 39 us (0.940)
  Pallas kernels: 40.8 us -> 38.3 us
    pallas_call x1, Pallas kernels: 40 us -> 37.5 us  [local(): pl.pallas_call(kernel, out_shape=(pltpu.VMEM((NC * 16, BS), F32), pltpu.V...]
where the time goes in v4:
time: 39 us; the launch traced here: 38.9 us
  Pallas kernels  38.3 us (98%)
  between operations  0.64 us (2%)
    pallas_call x1, Pallas kernels, local(): pl.pallas_call(kernel, out_shape=(pltpu.VMEM((NC * 16, BS), F32), pltpu.V...  37.5 us

profile of v4, /device:TPU:1, one launch (start us, length us, event | category | flops | bytes accessed | tf_op | source)
XLA Modules:
  0.0 38.9 jit_solution(2621801806325400282)
XLA Ops:
  0.6 37.5 %shard_map.86 = (f32[256,128]{1,0:T(8,128)S(1)}, f32[64,128]{1,0:T(8,128)S(1)}, f32[2,32,128]{2,1,0:T(8,128)S(1)}) custom-call(f32[32,2,128,128]{3,2,1,0:T(8,128)} %mat.1, s32[2,32]{1,0:T(2,128)} %bitcast.2, s32[1,32]{1,0:T(1,128)} %bitcast.3, f32[2,32,128]{2,1,0:T(8,128)} %xin.1, f32[2,32,128]{2,1,0:T(8,128)} %rhs.1, s32[2]{0:T(128)} %agg.1, ...), custom_call_target="tpu_custom_call" | custom-call | tf_op jit(solution)/shard_map/pallas_call | solution.py:288
  38.2 0.8 %shard_map.87 = (f32[8,32,128]{2,1,0:T(8,128)}, f32[2,32,128]{2,1,0:T(8,128)}) custom-call(f32[256,128]{1,0:T(8,128)S(1)} %get-tuple-element.5.cbuf, f32[64,128]{1,0:T(8,128)S(1)} %get-tuple-element.6.sqb, f32[2,32,128]{2,1,0:T(8,128)S(1)} %get-tuple-element.7.resid), custom_call_target="tpu_custom_call" | custom-call | tf_op jit(solution)/shard_map/pallas_call | solution.py:328

commit v5 on v4

--- a/solution.py
+++ b/solution.py
@@ -30,9 +30,9 @@
 
 def kernel(
     mat, cols, cnts, xin, rhs, agg, rest, cbuf, sqb, resid,
-    mraw, mw, xg, pout, pin, sb, rb, aout, ain, rhs_v, rest_v, rw, tmp, sqs, sqa,
+    mraw, mw, xg, pout, pin, sb, rb, aout, ain, rhs_v, rest_v, agg_v, rw, tmp, sqs, sqa,
     cols_s, cnts_s, agg_s,
-    mat_sem, loc_sem, ag_send, ag_recv, p_send, p_recv, s_send, s_recv,
+    mat_sem, loc_sem, ag_send, ag_recv, p_send, p_recv, s_send, s_recv, e_send, e_recv,
     a_send, a_recv, b_send, b_recv, o_send, o_recv, q_send, q_recv, tok,
 ):
     r = lax.axis_index("row")
@@ -78,8 +78,8 @@
         pltpu.make_async_copy(cols, cols_s, loc_sem.at[1]),
         pltpu.make_async_copy(cnts, cnts_s, loc_sem.at[2]),
         pltpu.make_async_copy(agg, agg_s, loc_sem.at[3]),
-        pltpu.make_async_copy(rhs, rhs_v, loc_sem.at[4]),
-        pltpu.make_async_copy(rest, rest_v, loc_sem.at[5]),
+        pltpu.make_async_copy(rhs, rhs_v.at[core], loc_sem.at[4]),
+        pltpu.make_async_copy(rest, rest_v.at[core], loc_sem.at[5]),
     ]
     for m in smalls:
         m.start()
@@ -136,9 +136,27 @@
     for m in smalls:
         m.wait()
     for k in range(2):
-        whi, wlo = split(rest_v[k])
-        rw[k, :, 0:BS] = whi
-        rw[k, :, BS:2 * BS] = wlo
+        agg_v[core, k] = jnp.full((8, BS), agg_s[k].astype(F32), F32)
+
+    def hand_over(i, ref):
+        return remote(ref.at[0], ref.at[0], e_send.at[i], e_recv.at[i], r, pair)
+
+    handed = [hand_over(i, ref) for i, ref in enumerate((rhs_v, rest_v, agg_v))]
+
+    @pl.when(core == 0)
+    def _():
+        for cp in handed:
+            cp.start()
+
+    @pl.when(core == 1)
+    def _():
+        for cp in handed:
+            cp.wait_recv()
+        for b in range(4):
+            whi, wlo = split(rest_v[b // 2, b % 2])
+            rw[b, :, 0:BS] = whi
+            rw[b, :, BS:2 * BS] = wlo
+
     for s in (1, -1):
         arrived(z_row(s))
         arrived(across(s))
@@ -174,100 +192,131 @@
         remote(pout.at[q], pin.at[q], p_send.at[i], p_recv.at[q], r, pair).wait_recv()
         for k in range(2):
             sb[q, k] = sb[q, k] + pin[q, k]
+        cp = remote(sb.at[q], rb.at[c], s_send.at[i], s_recv.at[c], r, q * 2 + 1)
         if d != (0, 0):
-            cp = remote(sb.at[q], rb.at[chip], s_send.at[i], s_recv.at[chip], r, q * 2 + core)
             cp.start()
             sends.append(cp)
-
-    total = [sb[chip, 0], sb[chip, 1]]
-    for d in Q_ORDER[:-1]:
-        q = chip_of(*d)
-        remote(sb.at[q], rb.at[q], s_send.at[0], s_recv.at[q], r, c).wait_recv()
-        for k in range(2):
-            total[k] = total[k] + rb[q, k]
-    contrib = []
-    sq = jnp.zeros((NV, BS), F32)
-    for k in range(2):
-        res = rhs_v[k] - total[k]
-        resid[k] = res
-        sq = sq + res * res
-        hi, lo = split(res)
-        o = lax.dot_general(
-            jnp.concatenate([hi, lo], axis=0), rw[k],
-            (((1,), (0,)), ((), ())), preferred_element_type=F32,
-        )
-        tmp[k] = o[:NV, :BS] + (o[:NV, BS:] + o[NV:, :BS])
-
-    eye = diagonal()
-    sq_row = jnp.sum(jnp.where(eye, jnp.sum(sq, axis=1, keepdims=True), 0.0), axis=0, keepdims=True)
-    for k in range(2):
-        for v in range(2):
-            aout[pl.ds(2 * k + v, NC, stride=8), :] = tmp[k, pl.ds(v, NC, stride=2), :]
-        aout[pl.ds(5 + k, NC, stride=8), :] = jnp.full((NC, BS), agg_s[k].astype(F32), F32)
-    aout[pl.ds(4, NC, stride=8), :] = jnp.broadcast_to(sq_row, (NC, BS))
-    aout[pl.ds(7, NC, stride=8), :] = jnp.zeros((NC, BS), F32)
-
-    sqs[...] = jnp.broadcast_to(sq_row, (8, BS))
+    last = cp
 
     def line(ref, j):
         return ref.at[pl.ds(pl.multiple_of(8 * j, 8), 1)]
 
-    def tile(ref, j):
-        return ref.at[pl.ds(pl.multiple_of(8 * j, 8), 8)]
-
-    for d in range(1, NC):
-        j = (c + d) % NC
-        cp = remote(tile(aout, j), tile(ain, c), a_send.at[d], a_recv.at[c], r, j)
+    def message(ref, j):
+        return ref.at[pl.ds(pl.multiple_of(24 * j, 8), 24)]
+
+    def slot(j):
+        return cbuf.at[pl.ds(pl.multiple_of(32 * j, 32), 32)]
+
+    def residual_to(col):
+        return remote(tmp.at[pl.ds(0, 2)], resid, e_send.at[3], e_recv.at[3], r, col)
+
+    @pl.when(core == 0)
+    def _():
+        last.start()
+        for cp in handed + [last]:
+            cp.wait_send()
+        residual_to(pair).wait_recv()
+        for d in range(NZ):
+            remote(line(sqb, d), line(sqb, d), q_send.at[0], q_recv.at[d], r, c).wait_recv()
+        for d in range(NQ):
+            remote(slot(d), slot(d), b_send.at[0], b_recv.at[d], r, c).wait_recv()
+
+    @pl.when(core == 1)
+    def _():
+        started = []
+
+        def start(*args):
+            cp = remote(*args)
+            cp.start()
+            started.append(cp)
+
+        total = [None, None, sb[chip, 0], sb[chip, 1]]
+        for d in Q_ORDER[::-1]:
+            for half in (1, 0):
+                if half == 1 and d == (0, 0):
+                    continue
+                j = chip_of(*d) * 2 + half
+                remote(sb.at[0], rb.at[j], s_send.at[0], s_recv.at[j], r, c).wait_recv()
+                for k in range(2):
+                    b = 2 * half + k
+                    total[b] = rb[j, k] if total[b] is None else total[b] + rb[j, k]
+        sq = jnp.zeros((NV, BS), F32)
+        for b in range(4):
+            res = rhs_v[b // 2, b % 2] - total[b]
+            if b < 2:
+                tmp[b] = res
+            else:
+                resid[b - 2] = res
+            sq = sq + res * res
+            hi, lo = split(res)
+            o = lax.dot_general(
+                jnp.concatenate([hi, lo], axis=0), rw[b],
+                (((1,), (0,)), ((), ())), preferred_element_type=F32,
+            )
+            tmp[2 + b] = o[:NV, :BS] + (o[:NV, BS:] + o[NV:, :BS])
+
+        sq_row = jnp.sum(
+            jnp.where(diagonal(), jnp.sum(sq, axis=1, keepdims=True), 0.0), axis=0, keepdims=True
+        )
+        for b in range(4):
+            for v in range(4):
+                aout[pl.ds(4 * b + v, NQ, stride=24), :] = tmp[2 + b, pl.ds(v, NQ, stride=4), :]
+            aout[pl.ds(17 + b, NQ, stride=24), :] = agg_v[b // 2, b % 2]
+        aout[pl.ds(16, NQ, stride=24), :] = jnp.broadcast_to(sq_row, (NQ, BS))
+        for b in range(21, 24):
+            aout[pl.ds(b, NQ, stride=24), :] = jnp.zeros((NQ, BS), F32)
+        sqs[...] = jnp.broadcast_to(sq_row, (8, BS))
+
+        for i, d in enumerate(Q_ORDER[:-1]):
+            q = chip_of(*d)
+            start(message(aout, q), message(ain, chip), a_send.at[i], a_recv.at[chip], r, q * 2 + 1)
+        for i, d in enumerate(Q_ORDER):
+            start(line(sqs, 0), line(sqa, chip), o_send.at[i], o_recv.at[chip], other, chip_of(*d) * 2 + 1)
+        cp = residual_to(pair)
         cp.start()
-        sends.append(cp)
-    for d in range(NC):
-        cp = remote(line(sqs, 0), line(sqa, c), o_send.at[d], o_recv.at[c], other, (c + d) % NC)
-        cp.start()
-        sends.append(cp)
-    tile(ain, c)[...] = tile(aout, c)[...]
-
-    who = lax.broadcasted_iota(jnp.int32, (NAGG, BS), 0).astype(F32)
-    acc = [jnp.zeros((NAGG, BS), F32) for _ in range(2)]
-    group_sq = jnp.zeros((1, BS), F32)
-    for d in range(NC):
-        j = (c + NC - d) % NC
-        if d > 0:
-            remote(tile(aout, j), tile(ain, j), a_send.at[0], a_recv.at[j], r, c).wait_recv()
-        t = tile(ain, j)[...]
-        for k in range(2):
-            sel = who == t[5 + k:6 + k, :]
-            for v in range(2):
-                acc[v] = acc[v] + jnp.where(sel, t[2 * k + v:2 * k + v + 1, :], 0.0)
-        group_sq = group_sq + t[4:5, :]
-
-    def slot(j):
-        return cbuf.at[pl.ds(pl.multiple_of(16 * j, 16), 16)]
-
-    slot(c)[0:8, :] = acc[0]
-    slot(c)[8:16, :] = acc[1]
-    for d in range(1, NC):
-        j = (c + d) % NC
-        cp = remote(slot(c), slot(c), b_send.at[d], b_recv.at[c], r, j)
-        cp.start()
-        sends.append(cp)
-
-    plane_sq = group_sq
-    for d in range(NC):
-        j = (c + NC - d) % NC
-        remote(line(sqs, 0), line(sqa, j), o_send.at[0], o_recv.at[j], r, c).wait_recv()
-        plane_sq = plane_sq + line(sqa, j)[...]
-    tile(sqb, z)[...] = jnp.broadcast_to(plane_sq, (8, BS))
-    for d in (4, 3, 5, 2, 6, 1, 7):
-        cp = remote(line(sqb, z), line(sqb, z), q_send.at[d], q_recv.at[z], z_row(d), c)
-        cp.start()
-        sends.append(cp)
-
-    for d in range(1, NZ):
-        j = (z + d) % NZ
-        remote(line(sqb, j), line(sqb, j), q_send.at[0], q_recv.at[j], r, c).wait_recv()
-    for d in range(1, NC):
-        j = (c + NC - d) % NC
-        remote(slot(j), slot(j), b_send.at[0], b_recv.at[j], r, c).wait_recv()
+        started.append(cp)
+
+        who = lax.broadcasted_iota(jnp.int32, (NAGG, BS), 0).astype(F32)
+        acc = [jnp.zeros((NAGG, BS), F32) for _ in range(4)]
+        plane_sq = jnp.zeros((1, BS), F32)
+        for d in Q_ORDER[::-1]:
+            q = chip_of(*d)
+            if d == (0, 0):
+                t = message(aout, q)[...]
+            else:
+                remote(message(aout, q), message(ain, q), a_send.at[0], a_recv.at[q], r, c).wait_recv()
+                t = message(ain, q)[...]
+            for b in range(4):
+                sel = who == t[17 + b:18 + b, :]
+                for v in range(4):
+                    acc[v] = acc[v] + jnp.where(sel, t[4 * b + v:4 * b + v + 1, :], 0.0)
+            plane_sq = plane_sq + t[16:17, :]
+        for v in range(4):
+            slot(chip)[8 * v:8 * v + 8, :] = acc[v]
+        for i, d in enumerate(Q_ORDER):
+            q = chip_of(*d)
+            start(slot(chip), slot(chip), b_send.at[2 * i], b_recv.at[chip], r, q * 2)
+            if d != (0, 0):
+                start(slot(chip), slot(chip), b_send.at[2 * i + 1], b_recv.at[chip], r, q * 2 + 1)
+
+        for d in Q_ORDER[::-1]:
+            q = chip_of(*d)
+            remote(line(sqs, 0), line(sqa, q), o_send.at[0], o_recv.at[q], r, c).wait_recv()
+            plane_sq = plane_sq + line(sqa, q)[...]
+        line(sqb, z)[...] = plane_sq
+        for i, d in enumerate((4, 3, 5, 2, 6, 1, 7, 0)):
+            start(line(sqb, z), line(sqb, z), q_send.at[2 * i], q_recv.at[z], z_row(d), chip * 2)
+            if d > 0:
+                start(line(sqb, z), line(sqb, z), q_send.at[2 * i + 1], q_recv.at[z], z_row(d), c)
+        for d in range(1, NZ):
+            j = (z + d) % NZ
+            remote(line(sqb, j), line(sqb, j), q_send.at[0], q_recv.at[j], r, c).wait_recv()
+        for d in Q_ORDER[:-1]:
+            q = chip_of(*d)
+            remote(slot(q), slot(q), b_send.at[0], b_recv.at[q], r, c).wait_recv()
+        for cp in started:
+            cp.wait_send()
+
     for cp in sends:
         cp.wait_send()
 
@@ -301,26 +350,28 @@
             pltpu.VMEM((NQ, 2, NV, BS), F32),
             pltpu.VMEM((NQ, 2, NV, BS), F32),
             pltpu.VMEM((NQ, 2, NV, BS), F32),
-            pltpu.VMEM((NQ, 2, NV, BS), F32),
-            pltpu.VMEM((NC * 8, BS), F32),
-            pltpu.VMEM((NC * 8, BS), F32),
-            pltpu.VMEM((2, NV, BS), F32),
-            pltpu.VMEM((2, BS, BS), F32),
-            pltpu.VMEM((2, BS, 2 * BS), BF16),
-            pltpu.VMEM((2, NV, BS), F32),
+            pltpu.VMEM((NC, 2, NV, BS), F32),
+            pltpu.VMEM((NQ * 24, BS), F32),
+            pltpu.VMEM((NQ * 24, BS), F32),
+            pltpu.VMEM((2, 2, NV, BS), F32),
+            pltpu.VMEM((2, 2, BS, BS), F32),
+            pltpu.VMEM((2, 2, 8, BS), F32),
+            pltpu.VMEM((4, BS, 2 * BS), BF16),
+            pltpu.VMEM((6, NV, BS), F32),
             pltpu.VMEM((8, BS), F32),
-            pltpu.VMEM((NC * 8, BS), F32),
+            pltpu.VMEM((NQ * 8, BS), F32),
             pltpu.SMEM((KB, GR), jnp.int32),
             pltpu.SMEM((1, GR), jnp.int32),
             pltpu.SMEM((2,), jnp.int32),
             dma((CHUNKS,)), dma((6,)),
             dma((24,)), dma((2 * NR,)),
             dma((NQ,)), dma((NQ,)),
+            dma((NQ,)), dma((NC,)),
+            dma((4,)), dma((4,)),
             dma((NQ,)), dma((NQ,)),
-            dma((NC,)), dma((NC,)),
-            dma((NC,)), dma((NC,)),
-            dma((NC,)), dma((NC,)),
-            dma((NZ,)), dma((NZ,)),
+            dma((NC,)), dma((NQ,)),
+            dma((NQ,)), dma((NQ,)),
+            dma((NC,)), dma((NZ,)),
             pltpu.SemaphoreType.REGULAR((3,)),
         ],
         compiler_params=pltpu.CompilerParams(collective_id=0, has_side_effects=True, vmem_limit_bytes=60 * 2**20),

time: 39 us -> 37.2 us (0.954)
  Pallas kernels: 38.3 us -> 36.5 us
    pallas_call x1, Pallas kernels: 37.5 us -> 35.7 us  [local(): pl.pallas_call(kernel, out_shape=(pltpu.VMEM((NC * 16, BS), F32), pltpu.V...]
where the time goes in v5:
time: 37.2 us; the launch traced here: 37.1 us
  Pallas kernels  36.5 us (98%)
  between operations  0.64 us (2%)
    pallas_call x1, Pallas kernels, local(): pl.pallas_call(kernel, out_shape=(pltpu.VMEM((NC * 16, BS), F32), pltpu.V...  35.7 us
    pallas_call x1, Pallas kernels, local(): pl.pallas_call(finish, out_shape=(jax.ShapeDtypeStruct((NAGG, NV, BS), F3...  0.77 us

profile of v5, /device:TPU:1, one launch (start us, length us, event | category | flops | bytes accessed | tf_op | source)
XLA Modules:
  0.0 37.1 jit_solution(8071923798282668653)
XLA Ops:
  0.6 35.7 %shard_map.86 = (f32[256,128]{1,0:T(8,128)S(1)}, f32[64,128]{1,0:T(8,128)S(1)}, f32[2,32,128]{2,1,0:T(8,128)S(1)}) custom-call(f32[32,2,128,128]{3,2,1,0:T(8,128)} %mat.1, s32[2,32]{1,0:T(2,128)} %bitcast.2, s32[1,32]{1,0:T(1,128)} %bitcast.3, f32[2,32,128]{2,1,0:T(8,128)} %xin.1, f32[2,32,128]{2,1,0:T(8,128)} %rhs.1, s32[2]{0:T(128)} %agg.1, ...), custom_call_target="tpu_custom_call" | custom-call | tf_op jit(solution)/shard_map/pallas_call | solution.py:337
  36.4 0.8 %shard_map.87 = (f32[8,32,128]{2,1,0:T(8,128)}, f32[2,32,128]{2,1,0:T(8,128)}) custom-call(f32[256,128]{1,0:T(8,128)S(1)} %get-tuple-element.5.cbuf, f32[64,128]{1,0:T(8,128)S(1)} %get-tuple-element.6.sqb, f32[2,32,128]{2,1,0:T(8,128)S(1)} %get-tuple-element.7.resid), custom_call_target="tpu_custom_call" | custom-call | tf_op jit(solution)/shard_map/pallas_call | solution.py:379

commit v6 on v5

--- a/solution.py
+++ b/solution.py
@@ -15,7 +15,9 @@
 GR, KB, NV, BS = 32, 2, 32, 128
 NAGG = 8
 CHUNKS = 4
-Q_ORDER = ((2, 1), (1, 1), (3, 1), (2, 0), (0, 1), (1, 0), (3, 0), (0, 0))
+Q_ORDER = ((2, 1), (2, 0), (1, 1), (3, 1), (0, 1), (1, 0), (3, 0), (0, 0))
+BATCH1 = 4
+BATCH2 = 4
 
 
 def split(x):
@@ -127,12 +129,12 @@
 
         def parts(g, carry):
             for s in range(KB):
-                hi, lo = split(mraw[g, s])
-                mw[g, 0:BS, s * BS:(s + 1) * BS] = hi
-                mw[g, BS:2 * BS, s * BS:(s + 1) * BS] = lo
+                hi, lo = split(mraw[g, s].T)
+                mw[g, s * BS:(s + 1) * BS, 0:BS] = hi
+                mw[g, s * BS:(s + 1) * BS, BS:2 * BS] = lo
             return carry
 
-        lax.fori_loop(k * per, (k + 1) * per, parts, 0)
+        lax.fori_loop(k * per, (k + 1) * per, parts, 0, unroll=4)
     for m in smalls:
         m.wait()
     for k in range(2):
@@ -173,29 +175,35 @@
         x = jnp.concatenate([xg[cols_s[0, g]], xg[cols_s[1, g]] * used], axis=1)
         hi, lo = split(x)
         o = lax.dot_general(
-            jnp.concatenate([hi, lo], axis=0), mw[g], (((1,), (1,)), ((), ())),
+            jnp.concatenate([hi, lo], axis=0), mw[g], (((1,), (0,)), ((), ())),
             preferred_element_type=F32,
         )
         return o[:NV, :BS] + (o[:NV, BS:] + o[NV:, :BS])
 
-    for i, d in enumerate(Q_ORDER):
-        q = chip_of(*d)
-        for k in range(2):
-            pout[q, k] = product(4 * q + 2 * (1 - core) + k)
-        cp = remote(pout.at[q], pin.at[q], p_send.at[i], p_recv.at[q], r, pair)
-        cp.start()
-        sends.append(cp)
-    for i, d in enumerate(Q_ORDER):
-        q = chip_of(*d)
-        for k in range(2):
-            sb[q, k] = product(4 * q + 2 * core + k)
-        remote(pout.at[q], pin.at[q], p_send.at[i], p_recv.at[q], r, pair).wait_recv()
-        for k in range(2):
-            sb[q, k] = sb[q, k] + pin[q, k]
-        cp = remote(sb.at[q], rb.at[c], s_send.at[i], s_recv.at[c], r, q * 2 + 1)
-        if d != (0, 0):
+    for first in range(0, NQ, BATCH1):
+        for d in Q_ORDER[first:first + BATCH1]:
+            q = chip_of(*d)
+            for k in range(2):
+                pout[q, k] = product(4 * q + 2 * (1 - core) + k)
+        for i in range(first, first + BATCH1):
+            q = chip_of(*Q_ORDER[i])
+            cp = remote(pout.at[q], pin.at[q], p_send.at[i], p_recv.at[q], r, pair)
             cp.start()
             sends.append(cp)
+    for first in range(0, NQ, BATCH2):
+        for d in Q_ORDER[first:first + BATCH2]:
+            q = chip_of(*d)
+            for k in range(2):
+                sb[q, k] = product(4 * q + 2 * core + k)
+        for i in range(first, first + BATCH2):
+            q = chip_of(*Q_ORDER[i])
+            remote(pout.at[q], pin.at[q], p_send.at[i], p_recv.at[q], r, pair).wait_recv()
+            for k in range(2):
+                sb[q, k] = sb[q, k] + pin[q, k]
+            cp = remote(sb.at[q], rb.at[c], s_send.at[i], s_recv.at[c], r, q * 2 + 1)
+            if i < NQ - 1:
+                cp.start()
+                sends.append(cp)
     last = cp
 
     def line(ref, j):
@@ -293,11 +301,10 @@
             plane_sq = plane_sq + t[16:17, :]
         for v in range(4):
             slot(chip)[8 * v:8 * v + 8, :] = acc[v]
+        for i, d in enumerate(Q_ORDER[:-1]):
+            start(slot(chip), slot(chip), b_send.at[2 * i + 1], b_recv.at[chip], r, chip_of(*d) * 2 + 1)
         for i, d in enumerate(Q_ORDER):
-            q = chip_of(*d)
-            start(slot(chip), slot(chip), b_send.at[2 * i], b_recv.at[chip], r, q * 2)
-            if d != (0, 0):
-                start(slot(chip), slot(chip), b_send.at[2 * i + 1], b_recv.at[chip], r, q * 2 + 1)
+            start(slot(chip), slot(chip), b_send.at[2 * i], b_recv.at[chip], r, chip_of(*d) * 2)
 
         for d in Q_ORDER[::-1]:
             q = chip_of(*d)

time: 37.2 us -> 36.6 us (0.984)
  Pallas kernels: 36.5 us -> 35.9 us
    pallas_call x1, Pallas kernels: 35.7 us -> 35.1 us  [local(): pl.pallas_call(kernel, out_shape=(pltpu.VMEM((NC * 16, BS), F32), pltpu.V...]
where the time goes in v6:
time: 36.6 us; the launch traced here: 36.5 us
  Pallas kernels  35.9 us (98%)
  between operations  0.64 us (2%)
    pallas_call x1, Pallas kernels, local(): pl.pallas_call(kernel, out_shape=(pltpu.VMEM((NC * 16, BS), F32), pltpu.V...  35.1 us
    pallas_call x1, Pallas kernels, local(): pl.pallas_call(finish, out_shape=(jax.ShapeDtypeStruct((NAGG, NV, BS), F3...  0.77 us

profile of v6, /device:TPU:1, one launch (start us, length us, event | category | flops | bytes accessed | tf_op | source)
XLA Modules:
  0.0 36.5 jit_solution(2515273779384079396)
XLA Ops:
  0.6 35.1 %shard_map.86 = (f32[256,128]{1,0:T(8,128)S(1)}, f32[64,128]{1,0:T(8,128)S(1)}, f32[2,32,128]{2,1,0:T(8,128)S(1)}) custom-call(f32[32,2,128,128]{3,2,1,0:T(8,128)} %mat.1, s32[2,32]{1,0:T(2,128)} %bitcast.2, s32[1,32]{1,0:T(1,128)} %bitcast.3, f32[2,32,128]{2,1,0:T(8,128)} %xin.1, f32[2,32,128]{2,1,0:T(8,128)} %rhs.1, s32[2]{0:T(128)} %agg.1, ...), custom_call_target="tpu_custom_call" | custom-call | tf_op jit(solution)/shard_map/pallas_call | solution.py:344
  35.7 0.8 %shard_map.87 = (f32[8,32,128]{2,1,0:T(8,128)}, f32[2,32,128]{2,1,0:T(8,128)}) custom-call(f32[256,128]{1,0:T(8,128)S(1)} %get-tuple-element.5.cbuf, f32[64,128]{1,0:T(8,128)S(1)} %get-tuple-element.6.sqb, f32[2,32,128]{2,1,0:T(8,128)S(1)} %get-tuple-element.7.resid), custom_call_target="tpu_custom_call" | custom-call | tf_op jit(solution)/shard_map/pallas_call | solution.py:386

commit v7 on v6

--- a/solution.py
+++ b/solution.py
@@ -301,10 +301,11 @@
             plane_sq = plane_sq + t[16:17, :]
         for v in range(4):
             slot(chip)[8 * v:8 * v + 8, :] = acc[v]
-        for i, d in enumerate(Q_ORDER[:-1]):
-            start(slot(chip), slot(chip), b_send.at[2 * i + 1], b_recv.at[chip], r, chip_of(*d) * 2 + 1)
-        for i, d in enumerate(Q_ORDER):
-            start(slot(chip), slot(chip), b_send.at[2 * i], b_recv.at[chip], r, chip_of(*d) * 2)
+        for i in range(NQ - 1):
+            q = i + (i + NQ - chip) // NQ
+            start(slot(chip), slot(chip), b_send.at[2 * i + 1], b_recv.at[chip], r, q * 2 + 1)
+        for i in range(NQ):
+            start(slot(chip), slot(chip), b_send.at[2 * i], b_recv.at[chip], r, i * 2)
 
         for d in Q_ORDER[::-1]:
             q = chip_of(*d)

time: 36.6 us -> 36.5 us (level)
  no operation moved by 1% of the time
where the time goes in v7:
time: 36.5 us; the launch traced here: 36.4 us
  Pallas kernels  35.8 us (98%)
  between operations  0.64 us (2%)
    pallas_call x1, Pallas kernels, local(): pl.pallas_call(kernel, out_shape=(pltpu.VMEM((NC * 16, BS), F32), pltpu.V...  35 us
    pallas_call x1, Pallas kernels, local(): pl.pallas_call(finish, out_shape=(jax.ShapeDtypeStruct((NAGG, NV, BS), F3...  0.77 us

profile of v7, /device:TPU:1, one launch (start us, length us, event | category | flops | bytes accessed | tf_op | source)
XLA Modules:
  0.0 36.4 jit_solution(1229040292599383292)
XLA Ops:
  0.6 35.0 %shard_map.86 = (f32[256,128]{1,0:T(8,128)S(1)}, f32[64,128]{1,0:T(8,128)S(1)}, f32[2,32,128]{2,1,0:T(8,128)S(1)}) custom-call(f32[32,2,128,128]{3,2,1,0:T(8,128)} %mat.1, s32[2,32]{1,0:T(2,128)} %bitcast.2, s32[1,32]{1,0:T(1,128)} %bitcast.3, f32[2,32,128]{2,1,0:T(8,128)} %xin.1, f32[2,32,128]{2,1,0:T(8,128)} %rhs.1, s32[2]{0:T(128)} %agg.1, ...), custom_call_target="tpu_custom_call" | custom-call | tf_op jit(solution)/shard_map/pallas_call | solution.py:345
  35.7 0.8 %shard_map.87 = (f32[8,32,128]{2,1,0:T(8,128)}, f32[2,32,128]{2,1,0:T(8,128)}) custom-call(f32[256,128]{1,0:T(8,128)S(1)} %get-tuple-element.5.cbuf, f32[64,128]{1,0:T(8,128)S(1)} %get-tuple-element.6.sqb, f32[2,32,128]{2,1,0:T(8,128)S(1)} %get-tuple-element.7.resid), custom_call_target="tpu_custom_call" | custom-call | tf_op jit(solution)/shard_map/pallas_call | solution.py:387
